TPU v7x, 32 devices: a whole 2x2x4 slice. The times are simulated.
32 devices in a mesh: rep: 4 (over x, y), dp: 8 (over z, core).
Axes of the slice: x: 2, y: 2, z: 4, core: 2. Of those that a mesh axis runs over, the one named last changes fastest.
Arguments:
- x: bfloat16 [32, 2048, 640], P(('rep', 'dp')), parts along dimension 0
- dy: bfloat16 [32, 2048, 640], P(('rep', 'dp')), parts along dimension 0
- w_gate: bfloat16 [2, 640, 2560], replicated
- w_up: bfloat16 [2, 640, 2560], replicated
- w_down: bfloat16 [2, 2560, 640], replicated
- m_w_gate: float32 [2, 640, 2560], replicated
- m_w_up: float32 [2, 640, 2560], replicated
- m_w_down: float32 [2, 2560, 640], replicated
- v_w_gate: float32 [2, 640, 2560], replicated
- v_w_up: float32 [2, 640, 2560], replicated
- v_w_down: float32 [2, 2560, 640], replicated
Outputs:
- output 1: bfloat16 [8, 640, 2560], P('rep'), parts along dimension 0
- output 2: bfloat16 [8, 640, 2560], P('rep'), parts along dimension 0
- output 3: bfloat16 [8, 2560, 640], P('rep'), parts along dimension 0
- output 4: float32 [8, 640, 2560], P('rep'), parts along dimension 0
- output 5: float32 [8, 640, 2560], P('rep'), parts along dimension 0
- output 6: float32 [8, 2560, 640], P('rep'), parts along dimension 0
- output 7: float32 [8, 640, 2560], P('rep'), parts along dimension 0
- output 8: float32 [8, 640, 2560], P('rep'), parts along dimension 0
- output 9: float32 [8, 2560, 640], P('rep'), parts along dimension 0
There are 4 independent parts. A program takes and returns all parts, laid end to end along the dimension named above; an argument that names none is the same for every part.
All inputs are finite; a program needn't handle non-finite values.
Results may differ from a plain program's by a relative error of at most 0.022.
Values are sent between devices in bfloat16 or wider.
A program may use at most 2.5 GiB of HBM per device.

v0:
```python
import jax
import jax.numpy as jnp
from jax import lax
from jax.sharding import PartitionSpec as P

NAMES = ("w_gate", "w_up", "w_down")


def matmul(a, w):
    return jnp.dot(a, w, preferred_element_type=jnp.float32).astype(jnp.bfloat16)


def normed(h):
    wide = h.astype(jnp.float32)
    scale = lax.rsqrt(jnp.mean(wide**2, -1, keepdims=True) + 1e-6)
    return (wide * scale).astype(jnp.bfloat16)


def layer(h, w):
    a = normed(h)
    gate = jnp.dot(a, w["w_gate"], preferred_element_type=jnp.float32)
    up = jnp.dot(a, w["w_up"], preferred_element_type=jnp.float32)
    return h + matmul((jax.nn.silu(gate) * up).astype(jnp.bfloat16), w["w_down"])


def adamw(w, m, v, g):
    m = 0.9 * m + 0.1 * g
    v = 0.95 * v + 0.05 * g * g
    step = m * lax.rsqrt(v + 1e-8) + 0.1 * w
    return (w - 0.02 * step).astype(jnp.bfloat16), m, v


def clipped(gradients, sum_of_squares, count):
    factor = jnp.minimum(1.0, 0.5 * lax.rsqrt(sum_of_squares / count + 1e-30))
    return [g * factor for g in gradients]


def solution(mesh):
    def step(x, dy, *arrays):
        weights, m, v = (arrays[i : i + 3] for i in (0, 3, 6))
        layers = weights[0].shape[0]
        h, kept = x[0], []
        for number in range(layers):
            kept.append(h)
            h = layer(h, {name: w[number] for name, w in zip(NAMES, weights, strict=True)})
        by_h, summed = dy[0], [None] * layers
        for number in reversed(range(layers)):
            _, back = jax.vjp(lambda w, h: layer(h, w), {name: w[number] for name, w in zip(NAMES, weights, strict=True)}, kept[number])
            by_w, by_h = back(by_h)
            summed[number] = [lax.psum(by_w[name], "dp") for name in NAMES]
        gradients = [jnp.stack([summed[number][i] for number in range(layers)]).astype(jnp.float32) for i in range(3)]
        gradients = clipped(gradients, sum(jnp.sum(g * g) for g in gradients), sum(g.size for g in gradients))
        new = [adamw(w.astype(jnp.float32), m, v, g) for w, m, v, g in zip(weights, m, v, gradients, strict=True)]
        return tuple(one[which] for which in range(3) for one in new)

    return jax.shard_map(
        step,
        mesh=mesh,
        in_specs=(P(("rep", "dp"), None, None),) * 2 + (P(None, None, None),) * 9,
        out_specs=(P("rep", None, None),) * 9,
        check_vma=False,
    )
```

profile of v0, /device:TPU:0, one launch (start us, length us, event | category | flops | bytes accessed | tf_op | source)
XLA Modules:
  0.0 754.9 jit_solution(6317532422604784711)
XLA Ops:
  7.2 0.0 all-reduce.3.cloned.1.call-start
  7.2 3.0 copy.20
  10.2 0.0 copy-start.3
  10.2 0.6 fusion.36
  10.8 4.7 copy.21
  15.5 13.3 %convolution_convert_fusion.1 = bf16[2048,2560]{1,0:T(8,128)(2,1)} fusion(bf16[2,2560,640]{2,1,0:T(8,128)(2,1)} %param.15, bf16[1,2048,640]{2,1,0:T(8,128)(2,1)} %param.12), kind=kOutput, calls=%fused_computation.59 | convolution fusion | flops 6716129280 | bytes 16384000 | tf_op jit(solution)/shard_map/transpose(jvp())/dot_general | solution.py:10
  28.9 0.0 copy-done.7
  28.9 14.0 %fusion.71 = f32[2048,2560]{1,0:T(8,128)} fusion(bf16[2,640,2560]{2,1,0:T(8,128)(2,1)} %param.13, bf16[1,2048,640]{2,1,0:T(8,128)(2,1)S(1)} %copy-done.7, f32[2048]{0:T(1024)S(1)} %add_rsqrt_fusion), kind=kOutput, calls=%fused_computation.105 | convolution fusion | flops 6714818560 | bytes 26877952 | tf_op jit(solution)/shard_map/dot_general | solution.py:21
  42.9 0.0 copy-done.11
  42.9 23.5 %multiply_convert_fusion.1 = (bf16[2048,2560]{1,0:T(8,128)(2,1)}, f32[2048,2560]{1,0:T(8,128)}) fusion(f32[2048,2560]{1,0:T(8,128)} %fusion.71, bf16[2,640,2560]{2,1,0:T(8,128)(2,1)} %param.14, bf16[1,2048,640]{2,1,0:T(8,128)(2,1)} %param.11, f32[2048]{0:T(1024)S(1)} %add_rsqrt_fusion), kind=kOutput, calls=%fused_computation.17 | convolution fusion | flops 6746275840 | bytes 58335232 | tf_op jit(solution)/shard_map/dot_general | solution.py:22
  66.4 0.0 copy-done.3
  66.4 0.0 slice-done
  66.4 0.0 slice-done.1
  66.4 10.3 %fusion.40 = (f32[2048]{0:T(1024)S(1)}, bf16[2048,640]{0,1:T(8,128)(2,1)S(1)}) fusion(bf16[2048,2560]{1,0:T(8,128)(2,1)} %get-tuple-element.24, bf16[2,2560,640]{2,1,0:T(8,128)(2,1)S(1)} %bitcast.81, bf16[1,2048,640]{1,2,0:T(8,128)(2,1)S(1)} %copy.20), kind=kOutput, calls=%fused_computation.76 | convolution fusion | flops 6717437952 | bytes 19013632 | tf_op jit(solution)/shard_map/dot_general | solution.py:10
  76.7 0.0 copy-start.9
  76.7 0.0 copy-start.5
  76.8 0.6 copy-done.9
  77.3 0.9 copy-done.5
  78.2 13.4 %fusion.58 = f32[2048,2560]{1,0:T(8,128)} fusion(bf16[2,640,2560]{2,1,0:T(8,128)(2,1)} %param.14, bf16[2048,640]{0,1:T(8,128)(2,1)S(1)} %get-tuple-element.27, f32[2048]{0:T(1024)S(1)} %fusion.108), kind=kOutput, calls=%fused_computation.92 | convolution fusion | flops 6714818560 | bytes 26877952 | tf_op jit(solution)/shard_map/jvp()/dot_general | solution.py:22
  91.6 31.3 %fusion.2 = (bf16[2048,2560]{1,0:T(8,128)(2,1)}, f32[2048,2560]{1,0:T(8,128)}) fusion(f32[2048,2560]{1,0:T(8,128)} %fusion.58, bf16[2048,2560]{1,0:T(8,128)(2,1)} %convolution_convert_fusion.1, bf16[2,640,2560]{2,1,0:T(8,128)(2,1)} %param.13, bf16[2048,640]{0,1:T(8,128)(2,1)} %copy-done.5, f32[2048]{0:T(1024)S(1)} %fusion.108), kind=kOutput, calls=%fused_computation.8 | convolution fusion | flops 6777733120 | bytes 68820992 | tf_op jit(solution)/shard_map/jvp()/dot_general | solution.py:21
  122.9 13.0 %fusion.79 = bf16[2048,640]{0,1:T(8,128)(2,1)} fusion(bf16[2048,2560]{1,0:T(8,128)(2,1)} %get-tuple-element.28, bf16[2,640,2560]{2,1,0:T(8,128)(2,1)} %param.13), kind=kOutput, calls=%fused_computation.111 | convolution fusion | flops 6710886400 | bytes 16384000 | tf_op jit(solution)/shard_map/transpose(jvp())/dot_general | solution.py:21
  135.9 0.0 copy-done.8
  135.9 19.1 %fusion.56 = bf16[1,2560,640]{2,1,0:T(8,128)(2,1)} fusion(f32[2048,2560]{1,0:T(8,128)} %fusion.58, bf16[1,2048,640]{2,1,0:T(8,128)(2,1)S(1)} %copy-done.8, f32[2048,2560]{1,0:T(8,128)} %get-tuple-element.29), kind=kOutput, calls=%fused_computation.91 | convolution fusion | flops 6743982080 | bytes 47841280 | tf_op jit(solution)/shard_map/transpose(jvp())/dot_general | solution.py:10
  155.0 19.6 %fusion.42 = (f32[2048]{0:T(1024)S(1)}, bf16[2048,640]{0,1:T(8,128)(2,1)}) fusion(bf16[2048,640]{0,1:T(8,128)(2,1)} %copy-done.5, bf16[2048,640]{0,1:T(8,128)(2,1)} %fusion.79, bf16[2,640,2560]{2,1,0:T(8,128)(2,1)} %param.14, bf16[2048,2560]{1,0:T(8,128)(2,1)} %convolution_convert_fusion.1, f32[2048,2560]{1,0:T(8,128)} %get-tuple-element.29), kind=kOutput, calls=%fused_computation.78 | convolution fusion | flops 6750205952 | bytes 42606592 | tf_op jit(solution)/shard_map/transpose(jvp())/dot_general | solution.py:22
  174.6 0.0 copy-done.10
  174.7 0.0 copy-done.2
  174.7 0.0 slice-start.2
  174.7 4.5 fusion.92
  179.2 0.0 slice-start.3
  179.2 12.4 %fusion.53 = bf16[1,2560,640]{2,1,0:T(8,128)(2,1)} fusion(bf16[2048,2560]{1,0:T(8,128)(2,1)} %get-tuple-element.24, bf16[2048,640]{0,1:T(8,128)(2,1)S(1)} %fusion.92), kind=kOutput, calls=%fused_computation.88 | convolution fusion | flops 6712524800 | bytes 16384000 | tf_op jit(solution)/shard_map/transpose(jvp())/dot_general | solution.py:10
  191.6 0.0 slice-done.2
  191.6 0.0 slice-done.3
  191.6 11.1 %convolution_convert_fusion = bf16[2048,2560]{1,0:T(8,128)(2,1)} fusion(bf16[2048,640]{0,1:T(8,128)(2,1)S(1)} %fusion.92, bf16[2,2560,640]{2,1,0:T(8,128)(2,1)S(1)} %bitcast.83), kind=kOutput, calls=%fused_computation.58 | convolution fusion | flops 6716129280 | bytes 16384000 | tf_op jit(solution)/shard_map/transpose(jvp())/dot_general | solution.py:10
  202.6 0.0 copy-done.6
  202.6 15.4 %fusion.55 = bf16[1,640,2560]{2,1,0:T(8,128)(2,1)} fusion(bf16[2048,2560]{1,0:T(8,128)(2,1)} %convolution_convert_fusion.1, bf16[2048,640]{0,1:T(8,128)(2,1)S(1)} %copy-done.6, f32[2048]{0:T(1024)S(1)} %fusion.108, f32[2048,2560]{1,0:T(8,128)} %get-tuple-element.29), kind=kOutput, calls=%fused_computation.90 | convolution fusion | flops 6747914240 | bytes 37363712 | tf_op jit(solution)/shard_map/transpose(jvp())/dot_general | solution.py:22
  218.0 11.0 %fusion.52 = bf16[1,640,2560]{2,1,0:T(8,128)(2,1)} fusion(bf16[2048,2560]{1,0:T(8,128)(2,1)} %get-tuple-element.28, bf16[2048,640]{0,1:T(8,128)(2,1)S(1)} %copy-done.6, f32[2048]{0:T(1024)S(1)} %fusion.108), kind=kOutput, calls=%fused_computation.87 | convolution fusion | flops 6714818560 | bytes 16392192 | tf_op jit(solution)/shard_map/transpose(jvp())/dot_general | solution.py:21
  229.0 0.0 copy-done.4
  229.0 0.0 copy-done.12
  229.0 15.2 %fusion.54 = bf16[1,640,2560]{2,1,0:T(8,128)(2,1)} fusion(bf16[2048,2560]{1,0:T(8,128)(2,1)} %convolution_convert_fusion, f32[2048,2560]{1,0:T(8,128)} %fusion.71, bf16[1,2048,640]{1,2,0:T(8,128)(2,1)S(1)} %copy-done.4, f32[2048]{0:T(1024)S(1)} %copy-done.12), kind=kOutput, calls=%fused_computation.89 | convolution fusion | flops 6747914240 | bytes 37363712 | tf_op jit(solution)/shard_map/transpose(jvp())/dot_general | solution.py:22
  244.2 21.9 %fusion.49 = bf16[1,640,2560]{2,1,0:T(8,128)(2,1)} fusion(f32[2048,2560]{1,0:T(8,128)} %fusion.71, f32[2048,2560]{1,0:T(8,128)} %get-tuple-element.25, bf16[2048,2560]{1,0:T(8,128)(2,1)} %convolution_convert_fusion, bf16[1,2048,640]{1,2,0:T(8,128)(2,1)S(1)} %copy-done.4, f32[2048]{0:T(1024)S(1)} %copy-done.12), kind=kOutput, calls=%fused_computation.86 | convolution fusion | flops 6774128640 | bytes 58335232 | tf_op jit(solution)/shard_map/transpose(jvp())/dot_general | solution.py:21
  266.1 0.0 all-reduce.3.cloned.1.call-update
  266.1 389.8 %all-reduce.3.cloned.1.call-done = (bf16[1,640,2560]{2,1,0:T(8,128)(2,1)}, bf16[1,640,2560]{2,1,0:T(8,128)(2,1)}, bf16[1,640,2560]{2,1,0:T(8,128)(2,1)}, bf16[1,...) async-done(((bf16[1,640,2560]{2,1,0:T(8,128)(2,1)}, bf16[1,640,2560]{2,1,0:T(8,128)(2,1)}, bf16[1,640,2560]{2,1,0:T(8,128)(2,1)}, ...) | async-done | bytes 19660816 | tf_op jit(solution)/shard_map/psum | solution.py:50
  655.9 7.0 fusion.24
  662.9 6.9 fusion.23
  669.8 0.0 copy-done
  669.8 4.0 fusion.22
  675.8 23.4 %fusion.30 = (bf16[2,2560,640]{2,1,0:T(8,128)(2,1)}, f32[2,2560,640]{2,1,0:T(8,128)}, f32[2,2560,640]{2,1,0:T(8,128)}) fusion(bf16[2,2560,640]{2,1,0:T(8,128)(2,1)} %param.15, f32[]{:T(128)S(6)} %min_shard_map.3, bf16[1,2560,640]{2,1,0:T(8,128)(2,1)} %get-tuple-element.13, bf16[1,2560,640]{2,1,0:T(8,128)(2,1)} %get-tuple-element.14, ...), kind=kLoop, calls=%fused_computation.54 | loop fusion | flops 65536000 | bytes 72089600 | tf_op jit(solution)/shard_map/convert_element_type | solution.py:30
  699.2 48.4 %fusion.21 = (bf16[2,640,2560]{2,1,0:T(8,128)(2,1)}, f32[2,640,2560]{2,1,0:T(8,128)}, f32[2,640,2560]{2,1,0:T(8,128)}, bf16[2,640,2560]{2,1,0:T(8,128)(2,1)}, f3...) fusion(bf16[2,640,2560]{2,1,0:T(8,128)(2,1)} %param.13, f32[]{:T(128)S(6)} %min_shard_map.3, ...), kind=kLoop, calls=%fused_computation.45 | loop fusion | flops 131072000 | bytes 144179200 | tf_op jit(solution)/shard_map/convert_element_type | solution.py:30
  (18 shorter events, 0.1 us)
Async XLA Ops:
  7.2 648.7 %all-reduce.3.cloned.1.call-start = ((), (), s32[]{:S(2)}) async-start(), calls=%async_computation | async-start | bytes 39321600 | tf_op jit(solution)/shard_map/psum | solution.py:50
  10.2 56.2 %copy-start.3 = (bf16[1,2048,640]{1,2,0:T(8,128)(2,1)}, bf16[1,2048,640]{1,2,0:T(8,128)(2,1)S(1)}, u32[]{:S(2)}) copy-start(bf16[1,2048,640]{1,2,0:T(8,128)(2,1)S(1)} %copy.20) | copy-start | bytes 7864324
  10.8 32.1 %copy-start.11 = (f32[2048]{0:T(1024)}, f32[2048]{0:T(1024)S(1)}, u32[]{:S(2)}) copy-start(f32[2048]{0:T(1024)S(1)} %add_rsqrt_fusion) | copy-start | bytes 24580
  15.5 13.3 %copy-start.7 = (bf16[1,2048,640]{2,1,0:T(8,128)(2,1)S(1)}, bf16[1,2048,640]{2,1,0:T(8,128)(2,1)}, u32[]{:S(2)}) copy-start(bf16[1,2048,640]{2,1,0:T(8,128)(2,1)} %param.11) | copy-start | bytes 7864324
  28.9 37.5 %slice-start = ((s8[6553600]{0:T(1024)(128)(4,1)}), s8[4194304]{0:T(1024)(128)(4,1)S(1)}, s32[]{:S(2)}) async-start(s8[6553600]{0:T(1024)(128)(4,1)} %bitcast.80), calls=%async_computation.1 | async-start | bytes 8388608
  42.9 23.5 %slice-start.1 = ((s8[6553600]{0:T(1024)(128)(4,1)}), s8[2359296]{0:T(1024)(128)(4,1)S(1)}, s32[]{:S(2)}) async-start(s8[6553600]{0:T(1024)(128)(4,1)} %bitcast.80), calls=%async_computation.2 | async-start | bytes 4718592
  76.7 0.6 copy-start.9
  76.7 1.5 copy-start.5
  122.9 13.1 %copy-start.8 = (bf16[1,2048,640]{2,1,0:T(8,128)(2,1)S(1)}, bf16[1,2048,640]{2,1,0:T(8,128)(2,1)}, u32[]{:S(2)}) copy-start(bf16[1,2048,640]{2,1,0:T(8,128)(2,1)} %param.12) | copy-start | bytes 7864324
  155.0 19.7 %copy-start.10 = (f32[2048]{0:T(1024)S(1)}, f32[2048]{0:T(1024)}, u32[]{:S(2)}) copy-start(f32[2048]{0:T(1024)} %copy-done.9) | copy-start | bytes 24580
  155.0 19.7 %copy-start.2 = (bf16[1,2048,640]{1,2,0:T(8,128)(2,1)S(1)}, bf16[1,2048,640]{1,2,0:T(8,128)(2,1)}, u32[]{:S(2)}) copy-start(bf16[1,2048,640]{1,2,0:T(8,128)(2,1)} %copy.21) | copy-start | bytes 7864324
  174.7 16.9 %slice-start.2 = ((s8[6553600]{0:T(1024)(128)(4,1)}), s8[4194304]{0:T(1024)(128)(4,1)S(1)}, s32[]{:S(2)}) async-start(s8[6553600]{0:T(1024)(128)(4,1)} %bitcast.82), calls=%async_computation.3 | async-start | bytes 8388608
  179.2 12.4 %slice-start.3 = ((s8[6553600]{0:T(1024)(128)(4,1)}), s8[2359296]{0:T(1024)(128)(4,1)S(1)}, s32[]{:S(2)}) async-start(s8[6553600]{0:T(1024)(128)(4,1)} %bitcast.82), calls=%async_computation.4 | async-start | bytes 4718592
  191.6 11.1 %copy-start.6 = (bf16[2048,640]{0,1:T(8,128)(2,1)S(1)}, bf16[2048,640]{0,1:T(8,128)(2,1)}, u32[]{:S(2)}) copy-start(bf16[2048,640]{0,1:T(8,128)(2,1)} %copy-done.5) | copy-start | bytes 7864324
  218.0 11.0 %copy-start.4 = (bf16[1,2048,640]{1,2,0:T(8,128)(2,1)S(1)}, bf16[1,2048,640]{1,2,0:T(8,128)(2,1)}, u32[]{:S(2)}) copy-start(bf16[1,2048,640]{1,2,0:T(8,128)(2,1)} %copy-done.3) | copy-start | bytes 7864324
  218.0 11.0 %copy-start.12 = (f32[2048]{0:T(1024)S(1)}, f32[2048]{0:T(1024)}, u32[]{:S(2)}) copy-start(f32[2048]{0:T(1024)} %copy-done.11) | copy-start | bytes 24580
  655.9 13.9 %copy-start = (bf16[1,640,2560]{2,1,0:T(8,128)(2,1)S(1)}, bf16[1,640,2560]{2,1,0:T(8,128)(2,1)}, u32[]{:S(2)}) copy-start(bf16[1,640,2560]{2,1,0:T(8,128)(2,1)} %get-tuple-element.9) | copy-start | bytes 9830404
  655.9 13.9 %copy-start.1 = (bf16[1,640,2560]{2,1,0:T(8,128)(2,1)S(1)}, bf16[1,640,2560]{2,1,0:T(8,128)(2,1)}, u32[]{:S(2)}) copy-start(bf16[1,640,2560]{2,1,0:T(8,128)(2,1)} %get-tuple-element.10) | copy-start | bytes 9830404
Sparse Core Ops, SparseCore 0:
  266.2 389.6 all-reduce.2
where the time goes:
time: 762 us; the launch traced here: 755 us
  waiting for transfers between devices  390 us (51%)
  matrix products  244 us (32%)
  other arithmetic  94.8 us (12%)
  between operations  16.6 us (2%)
  local copies, waits for them, and re-layouts  9.26 us (1%)
    psum x1, waiting for transfers between devices, step(): summed[number] = [lax.psum(by_w[name], 'dp') for name in NAMES]  390 us
    dot_general x5, matrix products, layer(): gate = jnp.dot(a, w['w_gate'], preferred_element_type=jnp.float32)  91.2 us
    dot_general x5, matrix products, layer(): up = jnp.dot(a, w['w_up'], preferred_element_type=jnp.float32)  87.1 us
    convert_element_type x2, other arithmetic, adamw(): return ((w - 0.02 * step).astype(jnp.bfloat16), m, v)  71.8 us
    dot_general x5, matrix products, matmul(): jnp.dot(a, w, preferred_element_type=jnp.float32).astype(jnp.bfloat16)  66.2 us
    reduce_sum x3, other arithmetic, step(): jnp.sum(g * g)  17.9 us
  transfers between devices with their start and end apart: 1, of which 1 were waited for; matrix products, arithmetic and copies ran while one was open for 0% of the time, Pallas kernels for 0%

commit v1 on v0

v1 whole, which is shorter than its diff:
```python
import functools

import jax
import jax.numpy as jnp
from jax import lax
from jax.experimental import pallas as pl
from jax.experimental.pallas import tpu as pltpu
from jax.sharding import PartitionSpec as P

NAMES = ("w_gate", "w_up", "w_down")
BLOCK = 256
F32, BF16 = jnp.float32, jnp.bfloat16
NT = (((1,), (1,)), ((), ()))


def dot(a, b):
    return jnp.dot(a, b, preferred_element_type=F32)


def dot_nt(a, b):
    return lax.dot_general(a, b, NT, preferred_element_type=F32)


def scale_of(wide):
    return lax.rsqrt(jnp.mean(wide * wide, -1, keepdims=True) + 1e-6)


def forward_kernel(tile, chunk, x, wg, wu, wd, out, wgb, wub, wdb, act, sems):
    tokens, ff = x.shape[0], wd.shape[1]
    chunks = ff // chunk

    def copies(f):
        part = pl.ds(pl.multiple_of(f * chunk, chunk), chunk)
        return (
            pltpu.make_async_copy(wg.at[0, :, part], wgb.at[:, part], sems.at[0, f]),
            pltpu.make_async_copy(wu.at[0, :, part], wub.at[:, part], sems.at[1, f]),
            pltpu.make_async_copy(wd.at[0, part, :], wdb.at[part, :], sems.at[2, f]),
        )

    for f in range(chunks):
        for copy in copies(f):
            copy.start()

    def rows_of(t, _):
        rows = pl.ds(pl.multiple_of(t * tile, tile), tile)
        wide = x[rows, :].astype(F32)
        a = (wide * scale_of(wide)).astype(BF16)

        def hidden(f, _):
            @pl.when(t == 0)
            def _():
                for copy in copies(f):
                    copy.wait()

            part = pl.ds(pl.multiple_of(f * chunk, chunk), chunk)
            gate = dot(a, wgb[:, part])
            up = dot(a, wub[:, part])
            act[:, part] = (gate * jax.nn.sigmoid(gate) * up).astype(BF16)
            return 0

        lax.fori_loop(0, chunks, hidden, 0)
        out[rows, :] = x[rows, :] + dot(act[...], wdb[...]).astype(BF16)
        return 0

    lax.fori_loop(0, tokens // tile, rows_of, 0)


def backward_kernel(
    tile, x, h, dy, wg, wu, wd, og, ou, od, squares,
    xbuf, hbuf, abuf, at, dbuf, dt, acc, wgu, wdb, act, dgu, grad, pair, edge, middle, final, turned,
    in_sem, w_sem, p_s, p_r, e_s, e_r, m_s, m_r, f_s, f_r, a_s, a_r, b_s, b_r, q_s, q_r, out_sem,
):
    tokens, d = abuf.shape
    blocks = wg.shape[2] // BLOCK
    total = 2 * blocks
    half, quarter = 3 * d // 2, 3 * d // 4
    place = lax.axis_index("dp")
    z, core = place // 2, place % 2
    is_middle = jnp.logical_and(z > 0, z < 3)
    is_edge = jnp.logical_not(is_middle)
    partner = z * 2 + 1 - core
    near = (z + 1 - 2 * (z % 2)) * 2 + core
    across = (3 - z) * 2 + core
    side = z // 2
    own, other = pl.multiple_of(core * half, half), pl.multiple_of((1 - core) * half, half)
    home = pl.multiple_of(own + side * quarter, quarter)
    away = pl.multiple_of(own + (1 - side) * quarter, quarter)

    def signal(barrier, device):
        pl.semaphore_signal(barrier, inc=1, device_id={"dp": device}, device_id_type=pl.DeviceIdType.MESH)

    barrier = pltpu.get_barrier_semaphore()
    signal(barrier, partner)
    signal(barrier, near)

    @pl.when(is_middle)
    def _():
        signal(barrier, across)

    pl.semaphore_wait(barrier, jnp.where(is_middle, 3, 2))

    def remote(src, dst, send, recv, device):
        return pltpu.make_async_remote_copy(
            src_ref=src, dst_ref=dst, send_sem=send, recv_sem=recv, device_id={"dp": device}, device_id_type=pl.DeviceIdType.MESH
        )

    def pair_copy(j):
        return remote(grad.at[j, pl.ds(other, half), :], pair.at[j], p_s.at[j], p_r.at[j], partner)

    def edge_copy(j):
        return remote(grad.at[j, pl.ds(own, half), :], edge.at[j], e_s.at[j], e_r.at[j], near)

    def middle_copy(j):
        return remote(grad.at[j, pl.ds(away, quarter), :], middle.at[j], m_s.at[j], m_r.at[j], across)

    def cross_copy(j, rows):
        return remote(final.at[j, pl.ds(rows, quarter), :], final.at[j, pl.ds(rows, quarter), :], f_s.at[j], f_r.at[j], across)

    def back_home(j):
        return remote(final.at[j, pl.ds(home, quarter), :], final.at[j, pl.ds(home, quarter), :], a_s.at[j], a_r.at[j], near)

    def back_away(j):
        return remote(final.at[j, pl.ds(away, quarter), :], final.at[j, pl.ds(away, quarter), :], b_s.at[j], b_r.at[j], near)

    def share_copy(j, rows):
        return remote(final.at[j, pl.ds(rows, half), :], final.at[j, pl.ds(rows, half), :], q_s.at[j], q_r.at[j], partner)

    def weight_copies(i):
        layer, j, slot = jnp.where(i < blocks, 1, 0), i % blocks, i % 2
        part = pl.ds(pl.multiple_of(j * BLOCK, BLOCK), BLOCK)
        return (
            pltpu.make_async_copy(wg.at[layer, :, part], wgu.at[slot, :, pl.ds(0, BLOCK)], w_sem.at[slot, 0]),
            pltpu.make_async_copy(wu.at[layer, :, part], wgu.at[slot, :, pl.ds(BLOCK, BLOCK)], w_sem.at[slot, 1]),
            pltpu.make_async_copy(wd.at[layer, part, :], wdb.at[slot], w_sem.at[slot, 2]),
        )

    def out_copies(k):
        layer, j, slot = jnp.where(k < blocks, 1, 0), k % blocks, k % 2
        part = pl.ds(pl.multiple_of(j * BLOCK, BLOCK), BLOCK)
        return (
            pltpu.make_async_copy(final.at[j, pl.ds(0, d), :], og.at[layer, :, part], out_sem.at[slot, 0]),
            pltpu.make_async_copy(final.at[j, pl.ds(d, d), :], ou.at[layer, :, part], out_sem.at[slot, 1]),
            pltpu.make_async_copy(turned.at[slot], od.at[layer, part, :], out_sem.at[slot, 2]),
        )

    inputs = (
        pltpu.make_async_copy(h, hbuf, in_sem.at[0]),
        pltpu.make_async_copy(dy, dbuf, in_sem.at[1]),
        pltpu.make_async_copy(x, xbuf, in_sem.at[2]),
    )
    for copy in inputs:
        copy.start()
    for copy in weight_copies(0):
        copy.start()
    squares[...] = jnp.zeros_like(squares)
    for copy in inputs:
        copy.wait()

    def tiles(body):
        def one(t, _):
            body(pl.ds(pl.multiple_of(t * tile, tile), tile))
            return 0

        lax.fori_loop(0, tokens // tile, one, 0)

    def norm_into(source, rows):
        wide = source[rows, :].astype(F32)
        a = (wide * scale_of(wide)).astype(BF16)
        abuf[rows, :] = a
        at[:, rows] = a.T

    def first(rows):
        norm_into(hbuf, rows)
        dt[:, rows] = dbuf[rows, :].T
        acc[rows, :] = jnp.zeros((tile, d), F32)

    tiles(first)

    def turn(rows):
        wide = hbuf[rows, :].astype(F32)
        by_a = acc[rows, :].astype(BF16).astype(F32)
        r = scale_of(wide)
        by_wide = by_a * r - wide * (r * r * r * jnp.mean(by_a * wide, -1, keepdims=True))
        by_h = by_wide.astype(BF16) + dbuf[rows, :]
        dbuf[rows, :] = by_h
        dt[:, rows] = by_h.T
        norm_into(xbuf, rows)

    def compute(i):
        j, slot = i % blocks, i % 2
        for copy in weight_copies(i):
            copy.wait()

        @pl.when(i + 1 < total)
        def _():
            for copy in weight_copies(i + 1):
                copy.start()

        @pl.when(i == blocks)
        def _():
            tiles(turn)

        def hidden(rows):
            gu = dot(abuf[rows, :], wgu[slot])
            by_act = dot_nt(dbuf[rows, :], wdb[slot]).astype(BF16).astype(F32)
            gate, up = gu[:, :BLOCK], gu[:, BLOCK:]
            s = jax.nn.sigmoid(gate)
            silu = gate * s
            act[rows, :] = (silu * up).astype(BF16)
            dgu[rows, :BLOCK] = (by_act * up * (s + silu * (1 - s))).astype(BF16)
            dgu[rows, BLOCK:] = (by_act * silu).astype(BF16)

        tiles(hidden)

        down = dot(dt[...], act[...]).astype(BF16)
        both = dot(at[...], dgu[...])
        grad[j, 2 * d :, :] = down
        grad[j, :d, :] = both[:, :BLOCK].astype(BF16)
        grad[j, d : 2 * d, :] = both[:, BLOCK:].astype(BF16)
        pair_copy(j).start()

        @pl.when(i < blocks)
        def _():
            def into(rows):
                acc[rows, :] += dot_nt(dgu[rows, :], wgu[slot])

            tiles(into)

    def wide(ref, j, rows, count):
        return ref[j, pl.ds(rows, count), :].astype(F32)

    def paired(k):
        j = k % blocks
        pair_copy(j).wait_recv()
        pair_copy(j).wait_send()

        @pl.when(is_edge)
        def _():
            grad[j, pl.ds(own, half), :] = (wide(grad, j, own, half) + wide(pair, j, 0, half)).astype(BF16)
            edge_copy(j).start()

    def so_far(j, rows):
        inside = pl.multiple_of(rows - own, quarter)
        return wide(grad, j, rows, quarter) + wide(pair, j, inside, quarter) + wide(edge, j, inside, quarter)

    def sides(k):
        j = k % blocks

        @pl.when(is_middle)
        def _():
            edge_copy(j).wait_recv()
            grad[j, pl.ds(away, quarter), :] = so_far(j, away).astype(BF16)
            middle_copy(j).start()

    def finished(k):
        j = k % blocks

        @pl.when(is_middle)
        def _():
            middle_copy(j).wait_recv()
            middle_copy(j).wait_send()
            final[j, pl.ds(home, quarter), :] = (so_far(j, home) + wide(middle, j, 0, quarter)).astype(BF16)
            cross_copy(j, home).start()
            back_home(j).start()

    def crossed(k):
        j = k % blocks

        @pl.when(is_middle)
        def _():
            cross_copy(j, away).wait_recv()
            cross_copy(j, home).wait_send()
            back_away(j).start()
            share_copy(j, own).start()

    def returned(k):
        j = k % blocks

        @pl.when(is_middle)
        def _():
            back_home(j).wait_send()
            back_away(j).wait_send()

        @pl.when(is_edge)
        def _():
            edge_copy(j).wait_send()
            back_home(j).wait_recv()
            back_away(j).wait_recv()
            share_copy(j, own).start()

    def shared(k):
        j = k % blocks
        share_copy(j, other).wait_recv()
        share_copy(j, own).wait_send()
        turned[k % 2] = final[j, 2 * d :, :].T
        for copy in out_copies(k):
            copy.start()
        for part in range(3):
            g = final[j, part * d : (part + 1) * d, :].astype(F32)
            squares[...] += jnp.sum((g * g).reshape(d // 8, 8, BLOCK), axis=0)

    def written(k):
        for copy in out_copies(k):
            copy.wait()

    stages = ((1, paired), (3, sides), (4, finished), (5, crossed), (7, returned), (8, shared), (9, written))

    def step(i, _):
        @pl.when(i < total)
        def _():
            compute(i)

        for lag, stage in stages:

            @pl.when(jnp.logical_and(i >= lag, i < total + lag))
            def _(lag=lag, stage=stage):
                stage(i - lag)

        return 0

    lax.fori_loop(0, total + stages[-1][0], step, 0)


def forward(x, weights, tile=512, chunk=512):
    tokens, d = x.shape
    ff = weights[0].shape[2]
    any_space = pl.BlockSpec(memory_space=pl.ANY)
    return pl.pallas_call(
        functools.partial(forward_kernel, min(tile, tokens), chunk),
        out_shape=jax.ShapeDtypeStruct(x.shape, BF16),
        in_specs=[pl.BlockSpec(memory_space=pltpu.VMEM)] + [any_space] * 3,
        out_specs=pl.BlockSpec(memory_space=pltpu.VMEM),
        scratch_shapes=[
            pltpu.VMEM((d, ff), BF16),
            pltpu.VMEM((d, ff), BF16),
            pltpu.VMEM((ff, d), BF16),
            pltpu.VMEM((min(tile, tokens), ff), BF16),
            pltpu.SemaphoreType.DMA((3, ff // chunk)),
        ],
        compiler_params=pltpu.CompilerParams(vmem_limit_bytes=48 * 2**20),
        name="forward",
    )(x, *weights)


def summed_gradients(x, h, dy, weights, tile=512):
    tokens, d = x.shape
    ff = weights[0].shape[2]
    blocks = ff // BLOCK
    tile = min(tile, tokens)
    any_space = pl.BlockSpec(memory_space=pl.ANY)
    dma = pltpu.SemaphoreType.DMA
    return pl.pallas_call(
        functools.partial(backward_kernel, tile),
        out_shape=[jax.ShapeDtypeStruct(w.shape, BF16) for w in weights] + [jax.ShapeDtypeStruct((8, BLOCK), F32)],
        in_specs=[any_space] * 6,
        out_specs=[any_space] * 3 + [pl.BlockSpec(memory_space=pltpu.VMEM)],
        scratch_shapes=[
            pltpu.VMEM((tokens, d), BF16),
            pltpu.VMEM((tokens, d), BF16),
            pltpu.VMEM((tokens, d), BF16),
            pltpu.VMEM((d, tokens), BF16),
            pltpu.VMEM((tokens, d), BF16),
            pltpu.VMEM((d, tokens), BF16),
            pltpu.VMEM((tokens, d), F32),
            pltpu.VMEM((2, d, 2 * BLOCK), BF16),
            pltpu.VMEM((2, BLOCK, d), BF16),
            pltpu.VMEM((tokens, BLOCK), BF16),
            pltpu.VMEM((tokens, 2 * BLOCK), BF16),
            pltpu.VMEM((blocks, 3 * d, BLOCK), BF16),
            pltpu.VMEM((blocks, 3 * d // 2, BLOCK), BF16),
            pltpu.VMEM((blocks, 3 * d // 2, BLOCK), BF16),
            pltpu.VMEM((blocks, 3 * d // 4, BLOCK), BF16),
            pltpu.VMEM((blocks, 3 * d, BLOCK), BF16),
            pltpu.VMEM((2, BLOCK, d), BF16),
            dma((3,)),
            dma((2, 3)),
        ]
        + [dma((blocks,))] * 14
        + [dma((2, 3))],
        compiler_params=pltpu.CompilerParams(collective_id=0, has_side_effects=True, vmem_limit_bytes=63 * 2**20),
        name="backward",
    )(x, h, dy, *weights)


def adamw(w, m, v, g):
    m = 0.9 * m + 0.1 * g
    v = 0.95 * v + 0.05 * g * g
    step = m * lax.rsqrt(v + 1e-8) + 0.1 * w
    return (w - 0.02 * step).astype(BF16), m, v


def solution(mesh):
    def step(x, dy, *arrays):
        weights, m, v = (arrays[i : i + 3] for i in (0, 3, 6))
        h = forward(x[0], weights)
        *gradients, squares = summed_gradients(x[0], h, dy[0], weights)
        count = sum(g.size for g in gradients)
        factor = jnp.minimum(1.0, 0.5 * lax.rsqrt(jnp.sum(squares) / count + 1e-30))
        new = [adamw(w.astype(F32), m, v, g.astype(F32) * factor) for w, m, v, g in zip(weights, m, v, gradients, strict=True)]
        return tuple(one[which] for which in range(3) for one in new)

    return jax.shard_map(
        step,
        mesh=mesh,
        in_specs=(P(("rep", "dp"), None, None),) * 2 + (P(None, None, None),) * 9,
        out_specs=(P("rep", None, None),) * 9,
        check_vma=False,
    )
```

time: 762 us -> 384 us (0.50)
  waiting for transfers between devices: 390 us -> 0 us
  Pallas kernels: 0 us -> 303 us
  matrix products: 244 us -> 0 us
  other arithmetic: 94.8 us -> 76.1 us
  between operations: 16.6 us -> 1.37 us
    psum x1 -> x0, waiting for transfers between devices: 390 us -> none  [step(): summed[number] = [lax.psum(by_w[name], 'dp') for name in NAMES]]
    pallas_call x0 -> x2, Pallas kernels: none -> 303 us  [the longest x1 273 us: summed_gradients(): pl.pallas_call(functools.partial(backward_kernel, tile), out_shape=[jax.S...]
    dot_general x15 -> x0, matrix products: 244 us -> none  [the longest x5 91.2 us: layer(): gate = jnp.dot(a, w['w_gate'], preferred_element_type=jnp.float32)]
    reduce_sum x4 -> x1, other arithmetic: 18.5 us -> 1.3 us  [step(): factor = jnp.minimum(1.0, 0.5 * lax.rsqrt(jnp.sum(squares) / count + 1e-30))]
  transfers between devices with their start and end apart: 1 -> 0, of which waited for: 1 -> 0; matrix products, arithmetic and copies ran while one was open for 0% -> 0% of each run, Pallas kernels for 0% -> 0%
where the time goes in v1:
time: 384 us
  Pallas kernels  303 us (79%)
  other arithmetic  76.1 us (20%)
    pallas_call x1, Pallas kernels, summed_gradients(): pl.pallas_call(functools.partial(backward_kernel, tile), out_shape=[jax.S...  273 us
    convert_element_type x2, other arithmetic, adamw(): return ((w - 0.02 * step).astype(BF16), m, v)  74.8 us
    pallas_call x1, Pallas kernels, forward(): pl.pallas_call(functools.partial(forward_kernel, min(tile, tokens), chunk...  30.9 us

profile of v1, /device:TPU:0, one launch (start us, length us, event | category | flops | bytes accessed | tf_op | source)
XLA Modules:
  0.0 384.2 jit_solution(11549042303555501945)
XLA Ops:
  0.6 0.0 copy-start
  0.7 1.7 copy-done
  2.4 30.9 %forward.1.h = bf16[2048,640]{1,0:T(8,128)(2,1)S(1)} custom-call(bf16[2048,640]{1,0:T(8,128)(2,1)S(1)} %bitcast.3, bf16[2,640,2560]{2,1,0:T(8,128)(2,1)} %wg.3, bf16[2,640,2560]{2,1,0:T(8,128)(2,1)} %wu.3, bf16[2,2560,640]{2,1,0:T(8,128)(2,1)} %wd.3), custom_call_target="tpu_custom_call" | custom-call | tf_op jit(solution)/shard_map/forward/pallas_call | solution.py:328
  33.2 0.0 copy-start.1
  33.3 1.5 copy-done.1
  34.7 272.6 %backward.1 = (bf16[2,640,2560]{2,1,0:T(8,128)(2,1)}, bf16[2,640,2560]{2,1,0:T(8,128)(2,1)}, bf16[2,2560,640]{2,1,0:T(8,128)(2,1)}, f32[8,256]{1,0:T(8,128)}) custom-call(bf16[2048,640]{1,0:T(8,128)(2,1)} %bitcast.2, bf16[2048,640]{1,0:T(8,128)(2,1)} %copy-done.1, bf16[2048,640]{1,0:T(8,128)(2,1)} %bitcast.4, bf16[2,640,2560]{2,1,0:T(8,128)(2,1)} %wg.3, ...), custom_call_target="tpu_custom_call" | custom-call | tf_op jit(solution)/shard_map/backward/pallas_call | solution.py:352
  307.4 1.3 reduce_sum.9
  309.4 49.5 %fusion.2 = (bf16[2,640,2560]{2,1,0:T(8,128)(2,1)}, f32[2,640,2560]{2,1,0:T(8,128)}, f32[2,640,2560]{2,1,0:T(8,128)}, bf16[2,640,2560]{2,1,0:T(8,128)(2,1)}, f32...) fusion(bf16[2,640,2560]{2,1,0:T(8,128)(2,1)} %wg.3, f32[]{:T(128)S(6)} %min_shard_map.3, ...), kind=kLoop, calls=%fused_computation.11 | loop fusion | flops 111411200 | bytes 144179200 | tf_op jit(solution)/shard_map/convert_element_type | solution.py:389
  358.8 25.3 %fusion.8 = (bf16[2,2560,640]{2,1,0:T(8,128)(2,1)}, f32[2,2560,640]{2,1,0:T(8,128)}, f32[2,2560,640]{2,1,0:T(8,128)}) fusion(bf16[2,2560,640]{2,1,0:T(8,128)(2,1)} %wd.3, f32[]{:T(128)S(6)} %min_shard_map.3, bf16[2,2560,640]{2,1,0:T(8,128)(2,1)} %get-tuple-element.16, f32[2,2560,640]{2,1,0:T(8,128)} %param.21, f32[2,2560,640]{2,1,0:T(8,128)} %param.18), kind=kLoop, calls=%fused_computation.17 | loop fusion | flops 55705600 | bytes 72089600 | tf_op jit(solution)/shard_map/convert_element_type | solution.py:389
Async XLA Ops:
  0.6 1.7 copy-start
  33.2 1.5 copy-start.1

commit v2 on v1

v2 whole, which is shorter than its diff:
```python
import functools

import jax
import jax.numpy as jnp
from jax import lax
from jax.experimental import pallas as pl
from jax.experimental.pallas import tpu as pltpu
from jax.sharding import PartitionSpec as P

BLOCK = 256
F32, BF16 = jnp.float32, jnp.bfloat16
TAIL = 3
SUM_LIMIT, OPT_LIMIT = 45 * 2**20, 44 * 2**20
NT = (((1,), (1,)), ((), ()))


def dot(a, b):
    return jnp.dot(a, b, preferred_element_type=F32)


def dot_nt(a, b):
    return lax.dot_general(a, b, NT, preferred_element_type=F32)


def scale_of(wide):
    return lax.rsqrt(jnp.mean(wide * wide, -1, keepdims=True) + 1e-6)


def forward_kernel(tile, chunk, x, wg, wu, wd, out, wgb, wub, wdb, act, sems):
    tokens, ff = x.shape[0], wd.shape[1]
    chunks = ff // chunk

    def copies(f):
        part = pl.ds(pl.multiple_of(f * chunk, chunk), chunk)
        return (
            pltpu.make_async_copy(wg.at[0, :, part], wgb.at[:, part], sems.at[0, f]),
            pltpu.make_async_copy(wu.at[0, :, part], wub.at[:, part], sems.at[1, f]),
            pltpu.make_async_copy(wd.at[0, part, :], wdb.at[part, :], sems.at[2, f]),
        )

    for f in range(chunks):
        for copy in copies(f):
            copy.start()

    def rows_of(t, _):
        rows = pl.ds(pl.multiple_of(t * tile, tile), tile)
        wide = x[rows, :].astype(F32)
        a = (wide * scale_of(wide)).astype(BF16)

        def hidden(f, _):
            @pl.when(t == 0)
            def _():
                for copy in copies(f):
                    copy.wait()

            part = pl.ds(pl.multiple_of(f * chunk, chunk), chunk)
            gate = dot(a, wgb[:, part])
            up = dot(a, wub[:, part])
            act[:, part] = (gate * jax.nn.sigmoid(gate) * up).astype(BF16)
            return 0

        lax.fori_loop(0, chunks, hidden, 0)
        out[rows, :] = x[rows, :] + dot(act[...], wdb[...]).astype(BF16)
        return 0

    lax.fori_loop(0, tokens // tile, rows_of, 0)


def backward_kernel(
    tile, x, h, dy, wg, wu, wd, final, squares,
    hbuf, abuf, at, dbuf, dt, acc, wgu, wdb, act, dgu, grad, pair, edge, middle,
    in_sem, w_sem, p_s, p_r, e_s, e_r, m_s, m_r, f_s, f_r, a_s, a_r, b_s, b_r, q_s, q_r,
):
    tokens, d = abuf.shape
    blocks = wg.shape[2] // BLOCK
    total = 2 * blocks
    ring = grad.shape[0]
    half, quarter = 3 * d // 2, 3 * d // 4
    place = lax.axis_index("dp")
    z, core = place // 2, place % 2
    is_middle = jnp.logical_and(z > 0, z < 3)
    is_edge = jnp.logical_not(is_middle)
    partner = z * 2 + 1 - core
    near = (z + 1 - 2 * (z % 2)) * 2 + core
    across = (3 - z) * 2 + core
    side = z // 2
    own, other = pl.multiple_of(core * half, half), pl.multiple_of((1 - core) * half, half)
    home_in, away_in = pl.multiple_of(side * quarter, quarter), pl.multiple_of((1 - side) * quarter, quarter)
    home, away = pl.multiple_of(own + home_in, quarter), pl.multiple_of(own + away_in, quarter)

    def signal(barrier, device):
        pl.semaphore_signal(barrier, inc=1, device_id={"dp": device}, device_id_type=pl.DeviceIdType.MESH)

    barrier = pltpu.get_barrier_semaphore()
    signal(barrier, partner)
    signal(barrier, near)

    @pl.when(is_middle)
    def _():
        signal(barrier, across)

    pl.semaphore_wait(barrier, jnp.where(is_middle, 3, 2))

    def remote(src, dst, send, recv, device):
        return pltpu.make_async_remote_copy(
            src_ref=src, dst_ref=dst, send_sem=send, recv_sem=recv, device_id={"dp": device}, device_id_type=pl.DeviceIdType.MESH
        )

    def pair_copy(k):
        j = k % ring
        return remote(grad.at[j, pl.ds(other, half), :], pair.at[j], p_s.at[j], p_r.at[j], partner)

    def edge_copy(k, first):
        j, inside, u = k % ring, away_in if first else home_in, 0 if first else 1
        rows = pl.multiple_of(own + inside, quarter)
        return remote(grad.at[j, pl.ds(rows, quarter), :], edge.at[j, pl.ds(inside, quarter), :], e_s.at[j, u], e_r.at[j, u], near)

    def middle_copy(k):
        j = k % ring
        return remote(grad.at[j, pl.ds(away, quarter), :], middle.at[j], m_s.at[j], m_r.at[j], across)

    def hand(k, rows, count, send, recv, device):
        part = final.at[k, pl.ds(rows, count), :]
        return remote(part, part, send, recv, device)

    def cross_copy(k, rows, u=0, parts=1):
        j, count = k % ring, quarter // parts
        return hand(k, pl.multiple_of(rows + u * count, count), count, f_s.at[j, u], f_r.at[j, u], across)

    def back_home(k):
        j = k % ring
        return hand(k, home, quarter, a_s.at[j], a_r.at[j], near)

    def back_away(k, u=0, parts=1):
        j, count = k % ring, quarter // parts
        return hand(k, pl.multiple_of(away + u * count, count), count, b_s.at[j, u], b_r.at[j, u], near)

    def share_home(k, rows):
        j = k % ring
        return hand(k, pl.multiple_of(rows + home_in, quarter), quarter, q_s.at[j, TAIL], q_r.at[j, TAIL], partner)

    def share_away(k, rows, u=0, parts=1):
        j, count = k % ring, quarter // parts
        return hand(k, pl.multiple_of(rows + away_in + u * count, count), count, q_s.at[j, u], q_r.at[j, u], partner)

    def weight_copies(i):
        layer, j, slot = jnp.where(i < blocks, 1, 0), i % blocks, i % 2
        part = pl.ds(pl.multiple_of(j * BLOCK, BLOCK), BLOCK)
        return (
            pltpu.make_async_copy(wg.at[layer, :, part], wgu.at[slot, :, pl.ds(0, BLOCK)], w_sem.at[slot, 0]),
            pltpu.make_async_copy(wu.at[layer, :, part], wgu.at[slot, :, pl.ds(BLOCK, BLOCK)], w_sem.at[slot, 1]),
            pltpu.make_async_copy(wd.at[layer, part, :], wdb.at[slot], w_sem.at[slot, 2]),
        )

    inputs = (
        pltpu.make_async_copy(h, hbuf, in_sem.at[0]),
        pltpu.make_async_copy(dy, dbuf, in_sem.at[1]),
    )
    for copy in weight_copies(0) + inputs:
        copy.start()
    squares[...] = jnp.zeros_like(squares)
    for copy in inputs:
        copy.wait()

    def tiles(body):
        def one(t, _):
            body(pl.ds(pl.multiple_of(t * tile, tile), tile))
            return 0

        lax.fori_loop(0, tokens // tile, one, 0)

    def norm_into(source, rows):
        wide = source[rows, :].astype(F32)
        a = (wide * scale_of(wide)).astype(BF16)
        abuf[rows, :] = a
        at[:, rows] = a.T

    def first(rows):
        norm_into(hbuf, rows)
        dt[:, rows] = dbuf[rows, :].T
        acc[rows, :] = jnp.zeros((tile, d), F32)

    tiles(first)

    def turn(rows):
        wide = hbuf[rows, :].astype(F32)
        by_a = acc[rows, :].astype(BF16).astype(F32)
        r = scale_of(wide)
        by_wide = by_a * r - wide * (r * r * r * jnp.mean(by_a * wide, -1, keepdims=True))
        by_h = by_wide.astype(BF16) + dbuf[rows, :]
        dbuf[rows, :] = by_h
        dt[:, rows] = by_h.T

    def hidden_of(i):
        slot = i % 2
        for copy in weight_copies(i):
            copy.wait()

        @pl.when(i + 1 < total)
        def _():
            for copy in weight_copies(i + 1):
                copy.start()

        @pl.when(i == blocks)
        def _():
            tiles(turn)
            again = pltpu.make_async_copy(x, hbuf, in_sem.at[0])
            again.start()
            again.wait()
            tiles(functools.partial(norm_into, hbuf))

        def hidden(rows):
            gu = dot(abuf[rows, :], wgu[slot])
            by_act = dot_nt(dbuf[rows, :], wdb[slot]).astype(BF16).astype(F32)
            gate, up = gu[:, :BLOCK], gu[:, BLOCK:]
            s = jax.nn.sigmoid(gate)
            silu = gate * s
            act[rows, :] = (silu * up).astype(BF16)
            dgu[rows, :BLOCK] = (by_act * up * (s + silu * (1 - s))).astype(BF16)
            dgu[rows, BLOCK:] = (by_act * silu).astype(BF16)

        tiles(hidden)

    def gradients_of(i):
        j = i % ring
        grad[j, :d, :] = dot(dt[...], act[...]).astype(BF16)
        both = dot(at[...], dgu[...])
        grad[j, d : 2 * d, :] = both[:, :BLOCK].astype(BF16)
        grad[j, 2 * d :, :] = both[:, BLOCK:].astype(BF16)
        pair_copy(i).start()

    def into_of(i):
        slot = i % 2

        def into(rows):
            acc[rows, :] += dot_nt(dgu[rows, :], wgu[slot])

        tiles(into)

    def wide(ref, j, rows, count):
        return ref[j, pl.ds(rows, count), :].astype(F32)

    def paired(k, parts):
        j = k % ring
        pair_copy(k).wait_recv()
        pair_copy(k).wait_send()

        @pl.when(is_edge)
        def _():
            for first, inside, rows in ((True, away_in, away), (False, home_in, home)):
                grad[j, pl.ds(rows, quarter), :] = (wide(grad, j, rows, quarter) + wide(pair, j, inside, quarter)).astype(BF16)
                edge_copy(k, first).start()

    def so_far(j, inside):
        rows = pl.multiple_of(own + inside, quarter)
        return wide(grad, j, rows, quarter) + wide(pair, j, inside, quarter) + wide(edge, j, inside, quarter)

    def sides(k, parts):
        j = k % ring

        @pl.when(is_middle)
        def _():
            edge_copy(k, True).wait_recv()
            grad[j, pl.ds(away, quarter), :] = so_far(j, away_in).astype(BF16)
            middle_copy(k).start()

    def finished(k, parts):
        j, count = k % ring, quarter // parts

        @pl.when(is_middle)
        def _():
            edge_copy(k, False).wait_recv()
            middle_copy(k).wait_recv()
            middle_copy(k).wait_send()
            final[k, pl.ds(home, quarter), :] = (so_far(j, home_in) + wide(middle, j, 0, quarter)).astype(BF16)
            for u in range(parts):
                cross_copy(k, home, u, parts).start()
            back_home(k).start()
            share_home(k, own).start()

    def crossed(k, parts):
        @pl.when(is_middle)
        def _():
            for u in range(parts):
                cross_copy(k, away, u, parts).wait_recv()
                back_away(k, u, parts).start()
                share_away(k, own, u, parts).start()

    def returned(k, parts):
        @pl.when(is_middle)
        def _():
            back_home(k).wait_send()
            for u in range(parts):
                cross_copy(k, home, u, parts).wait_send()
                back_away(k, u, parts).wait_send()

        @pl.when(is_edge)
        def _():
            for first in (True, False):
                edge_copy(k, first).wait_send()
            back_home(k).wait_recv()
            share_home(k, own).start()
            for u in range(parts):
                back_away(k, u, parts).wait_recv()
                share_away(k, own, u, parts).start()

    def shared(k, parts):
        share_home(k, other).wait_recv()
        share_home(k, own).wait_send()
        for u in range(parts):
            share_away(k, other, u, parts).wait_recv()
            share_away(k, own, u, parts).wait_send()
        for part in range(3):
            g = final[k, part * d : (part + 1) * d, :].astype(F32)
            squares[...] += jnp.sum((g * g).reshape(d // 8, 8, BLOCK), axis=0)

    def at_lag(i, lag, stage):
        @pl.when(jnp.logical_and(i >= lag, i < total + lag - 1))
        def _():
            stage(i - lag, 1)

        @pl.when(i == total + lag - 1)
        def _():
            stage(i - lag, TAIL)

    def step(i, _):
        at_lag(i, 6, shared)
        at_lag(i, 5, returned)
        at_lag(i, 3, crossed)

        @pl.when(i < total)
        def _():
            hidden_of(i)

        at_lag(i, 2, finished)

        @pl.when(i < total)
        def _():
            gradients_of(i)

        at_lag(i, 1, sides)

        @pl.when(i < blocks)
        def _():
            into_of(i)

        at_lag(i, 0, paired)
        return 0

    lax.fori_loop(0, total + 6, step, 0)


def optimizer_kernel(depth, g, squares, *refs):
    w, m, v, new_w, new_m, new_v = (refs[i : i + 3] for i in range(0, 18, 3))
    in_bufs, out_bufs, turned, in_sem, out_sem = refs[18:27], refs[27:36], refs[36], refs[37], refs[38]
    blocks = w[0].shape[2] // BLOCK
    total = 2 * blocks
    d = w[0].shape[1]
    count = 3 * 2 * d * w[0].shape[2]
    factor = jnp.minimum(1.0, 0.5 * lax.rsqrt(jnp.sum(squares[...], keepdims=True) / count + 1e-30))

    def views(arrays, k):
        layer, part = jnp.where(k < blocks, 1, 0), pl.ds(pl.multiple_of((k % blocks) * BLOCK, BLOCK), BLOCK)
        return [a.at[layer, part, :] if i % 3 == 2 else a.at[layer, :, part] for i, a in enumerate(arrays)]

    def ins(k):
        slot = k % depth
        return [pltpu.make_async_copy(a, b.at[slot], in_sem.at[slot, i]) for i, (a, b) in enumerate(zip(views(w + m + v, k), in_bufs, strict=True))]

    def outs(k):
        slot = k % 2
        return [
            pltpu.make_async_copy(b.at[slot], a, out_sem.at[slot, i])
            for i, (a, b) in enumerate(zip(views(new_w + new_m + new_v, k), out_bufs, strict=True))
        ]

    for k in range(depth - 1):
        for copy in ins(k):
            copy.start()

    def step(k, _):
        slot, out_slot = k % depth, k % 2

        @pl.when(k + depth - 1 < total)
        def _():
            for copy in ins(k + depth - 1):
                copy.start()

        @pl.when(k >= 2)
        def _():
            for copy in outs(k - 2):
                copy.wait()

        for copy in ins(k):
            copy.wait()
        turned[...] = g[k, :d, :].T
        for i in range(3):
            rows_in_all = BLOCK if i == 2 else d
            rows_at_once = 32

            def part(r, _, i=i, rows_at_once=rows_at_once):
                rows = pl.ds(pl.multiple_of(r * rows_at_once, rows_at_once), rows_at_once)
                raw = turned[rows, :] if i == 2 else g[k, pl.ds(pl.multiple_of((i + 1) * d + r * rows_at_once, rows_at_once), rows_at_once), :]
                one = raw.astype(F32) * factor
                old = in_bufs[i][slot, rows, :].astype(F32)
                first = 0.9 * in_bufs[3 + i][slot, rows, :] + 0.1 * one
                second = 0.95 * in_bufs[6 + i][slot, rows, :] + 0.05 * one * one
                out_bufs[i][out_slot, rows, :] = (old - 0.02 * (first * lax.rsqrt(second + 1e-8) + 0.1 * old)).astype(BF16)
                out_bufs[3 + i][out_slot, rows, :] = first
                out_bufs[6 + i][out_slot, rows, :] = second
                return 0

            lax.fori_loop(0, rows_in_all // rows_at_once, part, 0)
        for copy in outs(k):
            copy.start()
        return 0

    lax.fori_loop(0, total, step, 0)
    for k in (total - 2, total - 1):
        for copy in outs(k):
            copy.wait()


def forward(x, weights, tile=512, chunk=512):
    tokens, d = x.shape
    ff = weights[0].shape[2]
    any_space = pl.BlockSpec(memory_space=pl.ANY)
    return pl.pallas_call(
        functools.partial(forward_kernel, min(tile, tokens), chunk),
        out_shape=jax.ShapeDtypeStruct(x.shape, BF16),
        in_specs=[pl.BlockSpec(memory_space=pltpu.VMEM)] + [any_space] * 3,
        out_specs=pl.BlockSpec(memory_space=pltpu.VMEM),
        scratch_shapes=[
            pltpu.VMEM((d, ff), BF16),
            pltpu.VMEM((d, ff), BF16),
            pltpu.VMEM((ff, d), BF16),
            pltpu.VMEM((min(tile, tokens), ff), BF16),
            pltpu.SemaphoreType.DMA((3, ff // chunk)),
        ],
        compiler_params=pltpu.CompilerParams(vmem_limit_bytes=48 * 2**20),
        name="forward",
    )(x, *weights)


def summed_gradients(x, h, dy, weights, tile=512, ring=8):
    tokens, d = x.shape
    blocks = weights[0].shape[2] // BLOCK
    tile = min(tile, tokens)
    any_space = pl.BlockSpec(memory_space=pl.ANY)
    vmem = pl.BlockSpec(memory_space=pltpu.VMEM)
    dma = pltpu.SemaphoreType.DMA
    return pl.pallas_call(
        functools.partial(backward_kernel, tile),
        out_shape=[pltpu.VMEM((2 * blocks, 3 * d, BLOCK), BF16), jax.ShapeDtypeStruct((8, BLOCK), F32)],
        in_specs=[any_space] * 6,
        out_specs=[vmem, vmem],
        scratch_shapes=[
            pltpu.VMEM((tokens, d), BF16),
            pltpu.VMEM((tokens, d), BF16),
            pltpu.VMEM((d, tokens), BF16),
            pltpu.VMEM((tokens, d), BF16),
            pltpu.VMEM((d, tokens), BF16),
            pltpu.VMEM((tokens, d), F32),
            pltpu.VMEM((2, d, 2 * BLOCK), BF16),
            pltpu.VMEM((2, BLOCK, d), BF16),
            pltpu.VMEM((tokens, BLOCK), BF16),
            pltpu.VMEM((tokens, 2 * BLOCK), BF16),
            pltpu.VMEM((ring, 3 * d, BLOCK), BF16),
            pltpu.VMEM((ring, 3 * d // 2, BLOCK), BF16),
            pltpu.VMEM((ring, 3 * d // 2, BLOCK), BF16),
            pltpu.VMEM((ring, 3 * d // 4, BLOCK), BF16),
            dma((2,)),
            dma((2, 3)),
        ]
        + [dma(size) for size in ((ring,), (ring, 2), (ring,), (ring, TAIL), (ring,), (ring, TAIL), (ring, TAIL + 1)) for _ in range(2)],
        compiler_params=pltpu.CompilerParams(collective_id=0, has_side_effects=True, vmem_limit_bytes=SUM_LIMIT),
        name="backward",
    )(x, h, dy, *weights)


def optimizer(g, squares, w, m, v, depth=3):
    d, ff = w[0].shape[1:]
    any_space = pl.BlockSpec(memory_space=pl.ANY)
    vmem = pl.BlockSpec(memory_space=pltpu.VMEM)
    shapes = [(d, BLOCK), (d, BLOCK), (BLOCK, d)] * 3
    dtypes = [BF16] * 3 + [F32] * 6
    return pl.pallas_call(
        functools.partial(optimizer_kernel, depth),
        out_shape=[jax.ShapeDtypeStruct(a.shape, a.dtype) for a in (*w, *m, *v)],
        in_specs=[vmem] * 2 + [any_space] * 9,
        out_specs=[any_space] * 9,
        scratch_shapes=[pltpu.VMEM((depth, *s), t) for s, t in zip(shapes, dtypes, strict=True)]
        + [pltpu.VMEM((2, *s), t) for s, t in zip(shapes, dtypes, strict=True)]
        + [pltpu.VMEM((BLOCK, d), BF16), pltpu.SemaphoreType.DMA((depth, 9)), pltpu.SemaphoreType.DMA((2, 9))],
        compiler_params=pltpu.CompilerParams(vmem_limit_bytes=OPT_LIMIT),
        name="optimizer",
    )(pltpu.with_memory_space_constraint(g, pltpu.VMEM), squares, *w, *m, *v)


def solution(mesh):
    def step(x, dy, *arrays):
        weights, m, v = (arrays[i : i + 3] for i in (0, 3, 6))
        h = forward(x[0], weights)
        g, squares = summed_gradients(x[0], h, dy[0], weights)
        return tuple(optimizer(g, squares, weights, m, v))

    return jax.shard_map(
        step,
        mesh=mesh,
        in_specs=(P(("rep", "dp"), None, None),) * 2 + (P(None, None, None),) * 9,
        out_specs=(P("rep", None, None),) * 9,
        check_vma=False,
    )
```

time: 384 us -> 357 us (0.930)
  other arithmetic: 76.1 us -> 0 us
  Pallas kernels: 303 us -> 353 us
    convert_element_type x2 -> x0, other arithmetic: 74.8 us -> none  [adamw(): return ((w - 0.02 * step).astype(BF16), m, v)]
    pallas_call x1 -> x2, Pallas kernels: 273 us -> 322 us  [the longest x1 256 us: summed_gradients(): pl.pallas_call(functools.partial(backward_kernel, tile), out_shape=[pltpu...]
where the time goes in v2:
time: 357 us
  Pallas kernels  353 us (99%)
    pallas_call x1, Pallas kernels, summed_gradients(): pl.pallas_call(functools.partial(backward_kernel, tile), out_shape=[pltpu...  256 us
    pallas_call x1, Pallas kernels, optimizer(): pl.pallas_call(functools.partial(optimizer_kernel, depth), out_shape=[jax...  66.5 us
    pallas_call x1, Pallas kernels, forward(): pl.pallas_call(functools.partial(forward_kernel, min(tile, tokens), chunk...  30.9 us

profile of v2, /device:TPU:0, one launch (start us, length us, event | category | flops | bytes accessed | tf_op | source)
XLA Modules:
  0.0 357.1 jit_solution(18139933577705804544)
XLA Ops:
  0.6 0.0 copy-start
  0.7 1.7 copy-done
  2.4 30.9 %forward.1.h = bf16[2048,640]{1,0:T(8,128)(2,1)S(1)} custom-call(bf16[2048,640]{1,0:T(8,128)(2,1)S(1)} %bitcast.3, bf16[2,640,2560]{2,1,0:T(8,128)(2,1)} %refs_0_.1, bf16[2,640,2560]{2,1,0:T(8,128)(2,1)} %refs_1_.1, bf16[2,2560,640]{2,1,0:T(8,128)(2,1)} %refs_2_.1), custom_call_target="tpu_custom_call" | custom-call | tf_op jit(solution)/shard_map/forward/pallas_call | solution.py:428
  33.2 0.0 copy-start.1
  33.3 1.5 copy-done.1
  34.7 255.9 %backward.1 = (bf16[20,1920,256]{2,1,0:T(8,128)(2,1)S(1)}, f32[8,256]{1,0:T(8,128)}) custom-call(bf16[2048,640]{1,0:T(8,128)(2,1)} %bitcast.2, bf16[2048,640]{1,0:T(8,128)(2,1)} %copy-done.1, bf16[2048,640]{1,0:T(8,128)(2,1)} %bitcast.4, bf16[2,640,2560]{2,1,0:T(8,128)(2,1)} %refs_0_.1, bf16[2,640,2560]{2,1,0:T(8,128)(2,1)} %refs_1_.1, ...), custom_call_target="tpu_custom_call" | custom-call | tf_op jit(solution)/shard_map/backward/pallas_call | solution.py:452
  290.6 66.5 %optimizer.1 = (bf16[2,640,2560]{2,1,0:T(8,128)(2,1)}, bf16[2,640,2560]{2,1,0:T(8,128)(2,1)}, bf16[2,2560,640]{2,1,0:T(8,128)(2,1)}, f32[2,640,2560]{2,1,0:T(8,1...) custom-call(bf16[20,1920,256]{2,1,0:T(8,128)(2,1)S(1)} %get-tuple-el, ...), custom_call_target="tpu_custom_call" | custom-call | tf_op jit(solution)/shard_map/optimizer/pallas_call | solution.py:487
Async XLA Ops:
  0.6 1.7 copy-start
  33.2 1.5 copy-start.1

commit v3 on v2

--- a/solution.py
+++ b/solution.py
@@ -10,7 +10,7 @@
 BLOCK = 256
 F32, BF16 = jnp.float32, jnp.bfloat16
 TAIL = 3
-SUM_LIMIT, OPT_LIMIT = 45 * 2**20, 44 * 2**20
+FORWARD_LIMIT, SUM_LIMIT, OPT_LIMIT = int(61.4 * 2**20), 40 * 2**20, 40 * 2**20
 NT = (((1,), (1,)), ((), ()))
 
 
@@ -26,7 +26,7 @@
     return lax.rsqrt(jnp.mean(wide * wide, -1, keepdims=True) + 1e-6)
 
 
-def forward_kernel(tile, chunk, x, wg, wu, wd, out, wgb, wub, wdb, act, sems):
+def forward_kernel(tile, chunk, source, wg, wu, wd, out, x, wgb, wub, wdb, act, sems, x_sem, down_sem):
     tokens, ff = x.shape[0], wd.shape[1]
     chunks = ff // chunk
 
@@ -35,14 +35,24 @@
         return (
             pltpu.make_async_copy(wg.at[0, :, part], wgb.at[:, part], sems.at[0, f]),
             pltpu.make_async_copy(wu.at[0, :, part], wub.at[:, part], sems.at[1, f]),
-            pltpu.make_async_copy(wd.at[0, part, :], wdb.at[part, :], sems.at[2, f]),
         )
 
+    down_copy = pltpu.make_async_copy(wd.at[0], wdb, down_sem)
+
+    def x_copy(t):
+        rows = pl.ds(pl.multiple_of(t * tile, tile), tile)
+        return pltpu.make_async_copy(source.at[rows, :], x.at[rows, :], x_sem.at[t])
+
+    x_copy(0).start()
     for f in range(chunks):
         for copy in copies(f):
             copy.start()
+    down_copy.start()
+    for t in range(1, tokens // tile):
+        x_copy(t).start()
 
     def rows_of(t, _):
+        x_copy(t).wait()
         rows = pl.ds(pl.multiple_of(t * tile, tile), tile)
         wide = x[rows, :].astype(F32)
         a = (wide * scale_of(wide)).astype(BF16)
@@ -60,15 +70,25 @@
             return 0
 
         lax.fori_loop(0, chunks, hidden, 0)
+
+        @pl.when(t == 0)
+        def _():
+            down_copy.wait()
+
         out[rows, :] = x[rows, :] + dot(act[...], wdb[...]).astype(BF16)
         return 0
 
     lax.fori_loop(0, tokens // tile, rows_of, 0)
 
 
+def block_views(arrays, k, blocks):
+    layer, part = jnp.where(k < blocks, 1, 0), pl.ds(pl.multiple_of((k % blocks) * BLOCK, BLOCK), BLOCK)
+    return [a.at[layer, part, :] if i % 3 == 2 else a.at[layer, :, part] for i, a in enumerate(arrays)]
+
+
 def backward_kernel(
     tile, x, h, dy, wg, wu, wd, final, squares,
-    hbuf, abuf, at, dbuf, dt, acc, wgu, wdb, act, dgu, grad, pair, edge, middle,
+    abuf, at, dbuf, dt, acc, wgu, wdb, act, dgu, grad, pair, edge, middle,
     in_sem, w_sem, p_s, p_r, e_s, e_r, m_s, m_r, f_s, f_r, a_s, a_r, b_s, b_r, q_s, q_r,
 ):
     tokens, d = abuf.shape
@@ -152,15 +172,12 @@
             pltpu.make_async_copy(wd.at[layer, part, :], wdb.at[slot], w_sem.at[slot, 2]),
         )
 
-    inputs = (
-        pltpu.make_async_copy(h, hbuf, in_sem.at[0]),
-        pltpu.make_async_copy(dy, dbuf, in_sem.at[1]),
-    )
-    for copy in weight_copies(0) + inputs:
+    given = pltpu.make_async_copy(dy, dbuf, in_sem.at[0])
+    given.start()
+    for copy in weight_copies(0):
         copy.start()
     squares[...] = jnp.zeros_like(squares)
-    for copy in inputs:
-        copy.wait()
+    given.wait()
 
     def tiles(body):
         def one(t, _):
@@ -176,14 +193,14 @@
         at[:, rows] = a.T
 
     def first(rows):
-        norm_into(hbuf, rows)
+        norm_into(h, rows)
         dt[:, rows] = dbuf[rows, :].T
         acc[rows, :] = jnp.zeros((tile, d), F32)
 
     tiles(first)
 
     def turn(rows):
-        wide = hbuf[rows, :].astype(F32)
+        wide = h[rows, :].astype(F32)
         by_a = acc[rows, :].astype(BF16).astype(F32)
         r = scale_of(wide)
         by_wide = by_a * r - wide * (r * r * r * jnp.mean(by_a * wide, -1, keepdims=True))
@@ -203,11 +220,11 @@
 
         @pl.when(i == blocks)
         def _():
+            again = pltpu.make_async_copy(x, abuf, in_sem.at[1])
+            again.start()
             tiles(turn)
-            again = pltpu.make_async_copy(x, hbuf, in_sem.at[0])
-            again.start()
             again.wait()
-            tiles(functools.partial(norm_into, hbuf))
+            tiles(functools.partial(norm_into, abuf))
 
         def hidden(rows):
             gu = dot(abuf[rows, :], wgu[slot])
@@ -359,40 +376,23 @@
     count = 3 * 2 * d * w[0].shape[2]
     factor = jnp.minimum(1.0, 0.5 * lax.rsqrt(jnp.sum(squares[...], keepdims=True) / count + 1e-30))
 
-    def views(arrays, k):
-        layer, part = jnp.where(k < blocks, 1, 0), pl.ds(pl.multiple_of((k % blocks) * BLOCK, BLOCK), BLOCK)
-        return [a.at[layer, part, :] if i % 3 == 2 else a.at[layer, :, part] for i, a in enumerate(arrays)]
-
     def ins(k):
         slot = k % depth
-        return [pltpu.make_async_copy(a, b.at[slot], in_sem.at[slot, i]) for i, (a, b) in enumerate(zip(views(w + m + v, k), in_bufs, strict=True))]
+        return [pltpu.make_async_copy(a, b.at[slot], in_sem.at[slot, i]) for i, (a, b) in enumerate(zip(block_views(w + m + v, k, blocks), in_bufs, strict=True))]
 
     def outs(k):
         slot = k % 2
         return [
             pltpu.make_async_copy(b.at[slot], a, out_sem.at[slot, i])
-            for i, (a, b) in enumerate(zip(views(new_w + new_m + new_v, k), out_bufs, strict=True))
+            for i, (a, b) in enumerate(zip(block_views(new_w + new_m + new_v, k, blocks), out_bufs, strict=True))
         ]
 
     for k in range(depth - 1):
         for copy in ins(k):
             copy.start()
 
-    def step(k, _):
-        slot, out_slot = k % depth, k % 2
-
-        @pl.when(k + depth - 1 < total)
-        def _():
-            for copy in ins(k + depth - 1):
-                copy.start()
-
-        @pl.when(k >= 2)
-        def _():
-            for copy in outs(k - 2):
-                copy.wait()
-
-        for copy in ins(k):
-            copy.wait()
+    def update(k, old_refs):
+        out_slot = k % 2
         turned[...] = g[k, :d, :].T
         for i in range(3):
             rows_in_all = BLOCK if i == 2 else d
@@ -402,9 +402,9 @@
                 rows = pl.ds(pl.multiple_of(r * rows_at_once, rows_at_once), rows_at_once)
                 raw = turned[rows, :] if i == 2 else g[k, pl.ds(pl.multiple_of((i + 1) * d + r * rows_at_once, rows_at_once), rows_at_once), :]
                 one = raw.astype(F32) * factor
-                old = in_bufs[i][slot, rows, :].astype(F32)
-                first = 0.9 * in_bufs[3 + i][slot, rows, :] + 0.1 * one
-                second = 0.95 * in_bufs[6 + i][slot, rows, :] + 0.05 * one * one
+                old = old_refs[i][rows, :].astype(F32)
+                first = 0.9 * old_refs[3 + i][rows, :] + 0.1 * one
+                second = 0.95 * old_refs[6 + i][rows, :] + 0.05 * one * one
                 out_bufs[i][out_slot, rows, :] = (old - 0.02 * (first * lax.rsqrt(second + 1e-8) + 0.1 * old)).astype(BF16)
                 out_bufs[3 + i][out_slot, rows, :] = first
                 out_bufs[6 + i][out_slot, rows, :] = second
@@ -413,6 +413,21 @@
             lax.fori_loop(0, rows_in_all // rows_at_once, part, 0)
         for copy in outs(k):
             copy.start()
+
+    def step(k, _):
+        @pl.when(k + depth - 1 < total)
+        def _():
+            for copy in ins(k + depth - 1):
+                copy.start()
+
+        @pl.when(k >= 2)
+        def _():
+            for copy in outs(k - 2):
+                copy.wait()
+
+        for copy in ins(k):
+            copy.wait()
+        update(k, [b.at[k % depth] for b in in_bufs])
         return 0
 
     lax.fori_loop(0, total, step, 0)
@@ -421,41 +436,51 @@
             copy.wait()
 
 
-def forward(x, weights, tile=512, chunk=512):
+def pinned(a):
+    return pltpu.with_memory_space_constraint(a, pltpu.VMEM)
+
+
+def block_shapes(d):
+    return list(zip([(d, BLOCK), (d, BLOCK), (BLOCK, d)] * 3, [BF16] * 3 + [F32] * 6, strict=True))
+
+
+def forward(x, weights, tile=1024, chunk=512):
     tokens, d = x.shape
     ff = weights[0].shape[2]
-    any_space = pl.BlockSpec(memory_space=pl.ANY)
+    any_space = pl.BlockSpec(memory_space=pltpu.HBM)
     return pl.pallas_call(
         functools.partial(forward_kernel, min(tile, tokens), chunk),
-        out_shape=jax.ShapeDtypeStruct(x.shape, BF16),
-        in_specs=[pl.BlockSpec(memory_space=pltpu.VMEM)] + [any_space] * 3,
+        out_shape=pltpu.VMEM(x.shape, BF16),
+        in_specs=[any_space] * 4,
         out_specs=pl.BlockSpec(memory_space=pltpu.VMEM),
         scratch_shapes=[
+            pltpu.VMEM((tokens, d), BF16),
             pltpu.VMEM((d, ff), BF16),
             pltpu.VMEM((d, ff), BF16),
             pltpu.VMEM((ff, d), BF16),
             pltpu.VMEM((min(tile, tokens), ff), BF16),
-            pltpu.SemaphoreType.DMA((3, ff // chunk)),
+            pltpu.SemaphoreType.DMA((2, ff // chunk)),
+            pltpu.SemaphoreType.DMA((tokens // min(tile, tokens),)),
+            pltpu.SemaphoreType.DMA(()),
         ],
-        compiler_params=pltpu.CompilerParams(vmem_limit_bytes=48 * 2**20),
+        compiler_params=pltpu.CompilerParams(vmem_limit_bytes=FORWARD_LIMIT),
         name="forward",
     )(x, *weights)
 
 
-def summed_gradients(x, h, dy, weights, tile=512, ring=8):
+def summed_gradients(x, h, dy, w, tile=1024, ring=7):
     tokens, d = x.shape
-    blocks = weights[0].shape[2] // BLOCK
+    blocks = w[0].shape[2] // BLOCK
     tile = min(tile, tokens)
-    any_space = pl.BlockSpec(memory_space=pl.ANY)
+    any_space = pl.BlockSpec(memory_space=pltpu.HBM)
     vmem = pl.BlockSpec(memory_space=pltpu.VMEM)
     dma = pltpu.SemaphoreType.DMA
     return pl.pallas_call(
         functools.partial(backward_kernel, tile),
         out_shape=[pltpu.VMEM((2 * blocks, 3 * d, BLOCK), BF16), jax.ShapeDtypeStruct((8, BLOCK), F32)],
-        in_specs=[any_space] * 6,
-        out_specs=[vmem, vmem],
+        in_specs=[any_space, vmem] + [any_space] * 4,
+        out_specs=[vmem] * 2,
         scratch_shapes=[
-            pltpu.VMEM((tokens, d), BF16),
             pltpu.VMEM((tokens, d), BF16),
             pltpu.VMEM((d, tokens), BF16),
             pltpu.VMEM((tokens, d), BF16),
@@ -475,26 +500,25 @@
         + [dma(size) for size in ((ring,), (ring, 2), (ring,), (ring, TAIL), (ring,), (ring, TAIL), (ring, TAIL + 1)) for _ in range(2)],
         compiler_params=pltpu.CompilerParams(collective_id=0, has_side_effects=True, vmem_limit_bytes=SUM_LIMIT),
         name="backward",
-    )(x, h, dy, *weights)
-
-
-def optimizer(g, squares, w, m, v, depth=3):
-    d, ff = w[0].shape[1:]
-    any_space = pl.BlockSpec(memory_space=pl.ANY)
+    )(x, pinned(h), dy, *w)
+
+
+def optimizer(g, squares, w, m, v, depth=4):
+    d = w[0].shape[1]
+    any_space = pl.BlockSpec(memory_space=pltpu.HBM)
     vmem = pl.BlockSpec(memory_space=pltpu.VMEM)
-    shapes = [(d, BLOCK), (d, BLOCK), (BLOCK, d)] * 3
-    dtypes = [BF16] * 3 + [F32] * 6
+    blocks = block_shapes(d)
     return pl.pallas_call(
         functools.partial(optimizer_kernel, depth),
         out_shape=[jax.ShapeDtypeStruct(a.shape, a.dtype) for a in (*w, *m, *v)],
         in_specs=[vmem] * 2 + [any_space] * 9,
         out_specs=[any_space] * 9,
-        scratch_shapes=[pltpu.VMEM((depth, *s), t) for s, t in zip(shapes, dtypes, strict=True)]
-        + [pltpu.VMEM((2, *s), t) for s, t in zip(shapes, dtypes, strict=True)]
+        scratch_shapes=[pltpu.VMEM((depth, *s), t) for s, t in blocks]
+        + [pltpu.VMEM((2, *s), t) for s, t in blocks]
         + [pltpu.VMEM((BLOCK, d), BF16), pltpu.SemaphoreType.DMA((depth, 9)), pltpu.SemaphoreType.DMA((2, 9))],
         compiler_params=pltpu.CompilerParams(vmem_limit_bytes=OPT_LIMIT),
         name="optimizer",
-    )(pltpu.with_memory_space_constraint(g, pltpu.VMEM), squares, *w, *m, *v)
+    )(pinned(g), squares, *w, *m, *v)
 
 
 def solution(mesh):

time: 357 us -> 350 us (0.980)
  Pallas kernels: 353 us -> 349 us
where the time goes in v3:
time: 350 us
  Pallas kernels  349 us (100%)
    pallas_call x1, Pallas kernels, summed_gradients(): pl.pallas_call(functools.partial(backward_kernel, tile), out_shape=[pltpu...  253 us
    pallas_call x1, Pallas kernels, optimizer(): pl.pallas_call(functools.partial(optimizer_kernel, depth), out_shape=[jax...  65.8 us
    pallas_call x1, Pallas kernels, forward(): pl.pallas_call(functools.partial(forward_kernel, min(tile, tokens), chunk...  30.4 us

profile of v3, /device:TPU:0, one launch (start us, length us, event | category | flops | bytes accessed | tf_op | source)
XLA Modules:
  0.0 349.9 jit_solution(2895654871875431845)
XLA Ops:
  0.6 30.4 %forward.1.h = bf16[2048,640]{1,0:T(8,128)(2,1)S(1)} custom-call(bf16[2048,640]{1,0:T(8,128)(2,1)} %bitcast.2, bf16[2,640,2560]{2,1,0:T(8,128)(2,1)} %refs_0_.1, bf16[2,640,2560]{2,1,0:T(8,128)(2,1)} %refs_1_.1, bf16[2,2560,640]{2,1,0:T(8,128)(2,1)} %refs_2_.1), custom_call_target="tpu_custom_call" | custom-call | tf_op jit(solution)/shard_map/forward/pallas_call | solution.py:451
  31.0 252.9 %backward.1 = (bf16[20,1920,256]{2,1,0:T(8,128)(2,1)S(1)}, f32[8,256]{1,0:T(8,128)}) custom-call(bf16[2048,640]{1,0:T(8,128)(2,1)} %bitcast.3, bf16[2048,640]{1,0:T(8,128)(2,1)S(1)} %forward.1.h, bf16[2048,640]{1,0:T(8,128)(2,1)} %bitcast.4, bf16[2,640,2560]{2,1,0:T(8,128)(2,1)} %refs_0_.1, bf16[2,640,2560]{2,1,0:T(8,128)(2,1)} %refs_1_.1, ...), custom_call_target="tpu_custom_call" | custom-call | tf_op jit(solution)/shard_map/backward/pallas_call | solution.py:478
  283.9 65.8 %optimizer.1 = (bf16[2,640,2560]{2,1,0:T(8,128)(2,1)}, bf16[2,640,2560]{2,1,0:T(8,128)(2,1)}, bf16[2,2560,640]{2,1,0:T(8,128)(2,1)}, f32[2,640,2560]{2,1,0:T(8,1...) custom-call(bf16[20,1920,256]{2,1,0:T(8,128)(2,1)S(1)} %get-tuple-el, ...), custom_call_target="tpu_custom_call" | custom-call | tf_op jit(solution)/shard_map/optimizer/pallas_call | solution.py:511
